TPU v7x, 32 devices: a whole 2x2x4 slice. The times are simulated.
32 devices in a mesh: fsdp: 8 (over z, y), tp: 4 (over x, core).
Axes of the slice: x: 2, y: 2, z: 4, core: 2. Of those that a mesh axis runs over, the one named last changes fastest.
Arguments:
- tokens: bfloat16 [16384, 768], P(('fsdp', 'tp')), may hold values from -6 to 6
- pass_ids: int32 [16384], P(('fsdp', 'tp')), may hold values from 0 to 4
- prefix: int32 [8], P('fsdp'), may hold values from 0 to 2047
- cotangent: bfloat16 [16384, 768], P(('fsdp', 'tp')), may hold values from -6 to 6
- qkv_weight: bfloat16 [3, 768, 768], P(None, 'fsdp', 'tp'), may hold values from -0.21875 to 0.21875
- out_weight: bfloat16 [768, 768], P('tp', 'fsdp'), may hold values from -1.75 to 1.75
- fc1_weight: bfloat16 [768, 3072], P('fsdp', 'tp'), may hold values from -0.21875 to 0.21875
- fc2_weight: bfloat16 [3072, 768], P('tp', 'fsdp'), may hold values from -0.109375 to 0.109375
- ln1_gain: float32 [768], replicated, may hold values from 0.1 to 1.9
- ln1_bias: float32 [768], replicated, may hold values from -2 to 2
- qv_bias: float32 [2, 768], replicated, may hold values from -2 to 2
- out_bias: float32 [768], replicated, may hold values from -2 to 2
- ln2_gain: float32 [768], replicated, may hold values from 0.1 to 1.9
- ln2_bias: float32 [768], replicated, may hold values from -2 to 2
- fc1_bias: float32 [3072], replicated, may hold values from -3 to 3
- fc2_bias: float32 [768], replicated, may hold values from -2 to 2
- pass_table: float32 [5, 768], replicated, may hold values from -3 to 3
Outputs:
- activations: bfloat16 [16384, 768], P(('fsdp', 'tp'))
- input_grad: float32 [16384, 768], P(('fsdp', 'tp'))
- qkv_grad: float32 [3, 768, 768], P(None, 'fsdp', 'tp')
- out_grad: float32 [768, 768], P('tp', 'fsdp')
- fc1_grad: float32 [768, 3072], P('fsdp', 'tp')
- fc2_grad: float32 [3072, 768], P('tp', 'fsdp')
- ln1_gain_grad: float32 [768], replicated
- ln1_bias_grad: float32 [768], replicated
- qv_bias_grad: float32 [2, 768], replicated
- out_bias_grad: float32 [768], replicated
- ln2_gain_grad: float32 [768], replicated
- ln2_bias_grad: float32 [768], replicated
- fc1_bias_grad: float32 [3072], replicated
- fc2_bias_grad: float32 [768], replicated
- pass_table_grad: float32 [5, 768], replicated
All inputs are finite; a program needn't handle non-finite values.
Results may differ from a plain program's by a relative error of at most 0.009.
Values may be sent and summed in bfloat16 or wider, within the bound.
A program may use at most 128 MiB of HBM per device.

v0:
```python
from functools import partial
import jax
import jax.numpy as jnp
from jax import lax
from jax.sharding import PartitionSpec as P

HD = 64
NPASS = 5
QBLOCK = 512
HIGH = lax.Precision.HIGHEST
EPS = 1e-05
NEG_FILL = -1e30


def norm_forward(rows_in, gain, shift):
    center = rows_in - jnp.mean(rows_in, axis=-1, keepdims=True)
    scale_inv = lax.rsqrt(jnp.mean(center * center, axis=-1, keepdims=True) + EPS)
    unit_rows = center * scale_inv
    return (unit_rows * gain + shift, unit_rows, scale_inv)


def norm_backward(grad_out, unit_rows, scale_inv, gain):
    grad_unit = grad_out * gain
    first_mean = jnp.mean(grad_unit, axis=-1, keepdims=True)
    second_mean = jnp.mean(grad_unit * unit_rows, axis=-1, keepdims=True)
    grad_rows = scale_inv * (grad_unit - first_mean - unit_rows * second_mean)
    return (grad_rows, jnp.sum(grad_out * unit_rows, axis=0), jnp.sum(grad_out, axis=0))


def matmul_nt(left, right):
    return lax.dot_general(
        left, right, (((1,), (1,)), ((), ())), preferred_element_type=jnp.float32
    )


def matmul_tn(left, right):
    return lax.dot_general(
        left, right, (((0,), (0,)), ((), ())), preferred_element_type=jnp.float32
    )


def block_scores(query_block, keys_all, row_start, prefix_len, scale):
    raw = (
        jnp.einsum("qhe,khe->hqk", query_block, keys_all, preferred_element_type=jnp.float32)
        * scale
    )
    row_ids = row_start + jnp.arange(query_block.shape[0], dtype=jnp.int32)
    col_ids = jnp.arange(keys_all.shape[0], dtype=jnp.int32)
    allowed = (col_ids[None, :] <= row_ids[:, None]) | (col_ids[None, :] < prefix_len)
    return jnp.where(allowed[None], raw, NEG_FILL)


def attend_forward(queries, keys_all, values_all, prefix_len, scale):
    seq_len, heads_here, head_size = queries.shape
    block_count = seq_len // QBLOCK
    query_blocks = queries.reshape(block_count, QBLOCK, heads_here, head_size)
    block_starts = jnp.arange(block_count, dtype=jnp.int32) * QBLOCK

    def one_block(item):
        query_block, row_start = item
        masked = block_scores(query_block, keys_all, row_start, prefix_len, scale)
        peak = jnp.max(masked, axis=-1, keepdims=True)
        expo = jnp.exp(masked - peak)
        total_mass = jnp.sum(expo, axis=-1, keepdims=True)
        probs_low = (expo / total_mass).astype(jnp.bfloat16)
        out_block = jnp.einsum(
            "hqk,khe->qhe", probs_low, values_all, preferred_element_type=jnp.float32
        )
        return (out_block.astype(jnp.bfloat16), (peak + jnp.log(total_mass))[..., 0])

    outputs, log_mass = lax.map(one_block, (query_blocks, block_starts))
    return (outputs.reshape(seq_len, heads_here * head_size), log_mass)


def attend_backward(queries, keys_all, values_all, grad_mixed, log_mass, prefix_len, scale):
    seq_len, heads_here, head_size = queries.shape
    block_count = seq_len // QBLOCK
    query_blocks = queries.reshape(block_count, QBLOCK, heads_here, head_size)
    grad_blocks = grad_mixed.reshape(block_count, QBLOCK, heads_here, head_size)
    block_starts = jnp.arange(block_count, dtype=jnp.int32) * QBLOCK

    def one_block(carry, item):
        grad_keys, grad_values = carry
        query_block, grad_block, block_mass, row_start = item
        masked = block_scores(query_block, keys_all, row_start, prefix_len, scale)
        probs = jnp.exp(masked - block_mass[..., None])
        probs_low = probs.astype(jnp.bfloat16)
        grad_values = grad_values + jnp.einsum(
            "hqk,qhe->khe", probs_low, grad_block, preferred_element_type=jnp.float32
        )
        grad_probs = jnp.einsum(
            "qhe,khe->hqk", grad_block, values_all, preferred_element_type=jnp.float32
        )
        inner_sum = jnp.sum(probs * grad_probs, axis=-1, keepdims=True)
        grad_scores = (probs * (grad_probs - inner_sum)).astype(jnp.bfloat16)
        grad_query = (
            jnp.einsum("hqk,khe->qhe", grad_scores, keys_all, preferred_element_type=jnp.float32)
            * scale
        )
        grad_keys = (
            grad_keys
            + jnp.einsum(
                "hqk,qhe->khe", grad_scores, query_block, preferred_element_type=jnp.float32
            )
            * scale
        )
        return ((grad_keys, grad_values), grad_query)

    zero_state = jnp.zeros(keys_all.shape, jnp.float32)
    (grad_keys, grad_values), grad_queries = lax.scan(
        one_block, (zero_state, zero_state), (query_blocks, grad_blocks, log_mass, block_starts)
    )
    return (grad_queries.reshape(seq_len, heads_here, head_size), grad_keys, grad_values)


def on_device(
    tokens,
    pass_ids,
    prefix,
    cotangent,
    qkv_weight,
    out_weight,
    fc1_weight,
    fc2_weight,
    ln1_gain,
    ln1_bias,
    qv_bias,
    out_bias,
    ln2_gain,
    ln2_bias,
    fc1_bias,
    fc2_bias,
    pass_table,
):
    tp_count = lax.axis_size("tp")
    tp_rank = lax.axis_index("tp")
    local_rows = tokens.shape[0]
    seq_len = local_rows * tp_count
    cols_here = qkv_weight.shape[2]
    heads_here = cols_here // HD
    scale = HD ** (-0.5)
    prefix_len = prefix[0]
    gelu_tanh = partial(jax.nn.gelu, approximate=True)
    fsdp_count = lax.axis_size("fsdp")
    qkv_cols = lax.all_gather(qkv_weight, "fsdp", axis=1, tiled=True)
    qkv_full = qkv_cols
    hidden_here = fc1_weight.shape[1]
    qv_here = lax.dynamic_slice_in_dim(qv_bias, tp_rank * cols_here, cols_here, 1)
    one_hot = (pass_ids[:, None] == jnp.arange(NPASS, dtype=jnp.int32)[None, :]).astype(jnp.float32)
    block_in = tokens.astype(jnp.float32) + jnp.dot(
        one_hot, pass_table, precision=HIGH, preferred_element_type=jnp.float32
    )
    normed, unit_one, inv_one = norm_forward(block_in, ln1_gain, ln1_bias)
    normed_all = lax.all_gather(normed.astype(jnp.bfloat16), "tp", axis=0, tiled=True)
    out_pieces = lax.all_gather(out_weight, ("fsdp", "tp"), axis=0, tiled=False)
    out_pieces = out_pieces.reshape((fsdp_count, tp_count) + out_weight.shape)
    out_all = jnp.transpose(out_pieces, (1, 2, 0, 3)).reshape(
        tp_count * out_weight.shape[0], fsdp_count * out_weight.shape[1]
    )
    out_full = lax.dynamic_slice_in_dim(
        out_all, tp_rank * out_weight.shape[0], out_weight.shape[0], 0
    )
    shards = (fc1_weight, fc2_weight)
    packed = jnp.concatenate([piece.reshape(-1) for piece in shards])
    packed, qkv_cols, normed_all = lax.optimization_barrier((packed, qkv_cols, normed_all))
    qkv_full = qkv_cols
    gathered = lax.all_gather(packed, "fsdp", axis=0, tiled=False)
    qkv_all = lax.all_gather(qkv_cols, "tp", axis=2, tiled=True)
    grad_rows = lax.all_gather(cotangent, "tp", axis=0, tiled=True)
    projected = jnp.einsum("rd,kdc->krc", normed_all, qkv_full, preferred_element_type=jnp.float32)
    queries = (projected[0] + qv_here[0]).astype(jnp.bfloat16).reshape(seq_len, heads_here, HD)
    keys_all = projected[1].astype(jnp.bfloat16).reshape(seq_len, heads_here, HD)
    values_all = (projected[2] + qv_here[1]).astype(jnp.bfloat16).reshape(seq_len, heads_here, HD)
    mixed, log_mass = attend_forward(queries, keys_all, values_all, prefix_len, scale)
    mixed, grad_rows, gathered = lax.optimization_barrier((mixed, grad_rows, gathered))
    pieces = []
    offset = 0
    for piece in shards:
        size = piece.size
        pieces.append(gathered[:, offset : offset + size].reshape((fsdp_count,) + piece.shape))
        offset += size
    fc1_part = pieces[0].reshape(-1, fc1_weight.shape[1])
    fc2_part = jnp.moveaxis(pieces[1], 0, 1).reshape(fc2_weight.shape[0], -1)
    mixed_rows = lax.all_to_all(mixed, "tp", 0, 1, tiled=True)
    middle = block_in + jnp.dot(mixed_rows, out_all, preferred_element_type=jnp.float32) + out_bias
    normed_two, unit_two, inv_two = norm_forward(middle, ln2_gain, ln2_bias)
    normed_two = normed_two.astype(jnp.bfloat16)
    grad_top = cotangent.astype(jnp.float32)
    fc1_bias_here = lax.dynamic_slice_in_dim(fc1_bias, tp_rank * hidden_here, hidden_here, 0)
    normed_rows = lax.all_gather(normed_two, "tp", axis=0, tiled=True)
    before = jnp.dot(normed_rows, fc1_part, preferred_element_type=jnp.float32) + fc1_bias_here
    hidden = gelu_tanh(before).astype(jnp.bfloat16)
    fc2_partial = jnp.dot(hidden, fc2_part, preferred_element_type=jnp.float32).astype(jnp.bfloat16)
    grad_hidden = matmul_nt(grad_rows, fc2_part)
    grad_before = jax.vjp(gelu_tanh, before)[1](grad_hidden)[0].astype(jnp.bfloat16)
    grad_fc1_bias = lax.dynamic_update_slice_in_dim(
        jnp.zeros(fc1_bias.shape, jnp.float32),
        jnp.sum(grad_before.astype(jnp.float32), axis=0),
        tp_rank * hidden_here,
        0,
    )
    grad_fc1 = matmul_tn(normed_rows, grad_before)
    grad_fc2 = matmul_tn(hidden, grad_rows)
    grad_normed_two = lax.psum_scatter(
        matmul_nt(grad_before, fc1_part), "tp", scatter_dimension=0, tiled=True
    )
    grad_normed_two, fc2_partial, grad_fc1, grad_fc2 = lax.optimization_barrier(
        (grad_normed_two, fc2_partial, grad_fc1, grad_fc2)
    )
    grad_fc2_bias = jnp.sum(grad_top, axis=0)
    grad_from_norm, grad_ln2_gain, grad_ln2_bias = norm_backward(
        grad_normed_two, unit_two, inv_two, ln2_gain
    )
    grad_middle = grad_top + grad_from_norm
    grad_out_bias = jnp.sum(grad_middle, axis=0)
    grad_attn_rows = lax.all_gather(grad_middle.astype(jnp.bfloat16), "tp", axis=0, tiled=True)
    fc2_partial, grad_attn_rows = lax.optimization_barrier((fc2_partial, grad_attn_rows))
    result = (
        middle
        + lax.psum_scatter(fc2_partial, "tp", scatter_dimension=0, tiled=True).astype(jnp.float32)
        + fc2_bias
    )
    grad_out_w = matmul_tn(mixed, grad_attn_rows)
    fsdp_count = lax.axis_size("fsdp")
    dense_grads = (
        jnp.moveaxis(grad_out_w.reshape(grad_out_w.shape[0], fsdp_count, -1), 1, 0),
        grad_fc1.reshape(fsdp_count, -1, grad_fc1.shape[1]),
        jnp.moveaxis(grad_fc2.reshape(grad_fc2.shape[0], fsdp_count, -1), 1, 0),
    )
    dense_packed = jnp.concatenate([g.reshape(fsdp_count, -1) for g in dense_grads], axis=1)
    dense_summed = lax.psum_scatter(
        dense_packed.reshape(-1, grad_fc1.shape[1]), "fsdp", scatter_dimension=0, tiled=True
    ).reshape(1, -1)
    grad_mixed = (
        matmul_nt(grad_attn_rows, out_full).astype(jnp.bfloat16).reshape(seq_len, heads_here, HD)
    )
    grad_queries, grad_keys, grad_values = attend_backward(
        queries, keys_all, values_all, grad_mixed, log_mass, prefix_len, scale
    )
    grad_q_low = grad_queries.astype(jnp.bfloat16).reshape(seq_len, cols_here)
    grad_k_low = grad_keys.astype(jnp.bfloat16).reshape(seq_len, cols_here)
    grad_v_low = grad_values.astype(jnp.bfloat16).reshape(seq_len, cols_here)
    grad_proj = jnp.stack([grad_q_low, grad_k_low, grad_v_low], axis=1)
    grad_proj, result, dense_summed = lax.optimization_barrier((grad_proj, result, dense_summed))
    dense_shards = []
    offset = 0
    for g in dense_grads:
        size = g[0].size
        dense_shards.append(dense_summed[0, offset : offset + size].reshape(g.shape[1:]))
        offset += size
    out_shard, fc1_shard, fc2_shard = dense_shards
    grad_qv_here = jnp.stack(
        [
            jnp.sum(grad_q_low.astype(jnp.float32), axis=0),
            jnp.sum(grad_v_low.astype(jnp.float32), axis=0),
        ],
        axis=0,
    )
    grad_qv_bias = lax.dynamic_update_slice_in_dim(
        jnp.zeros(qv_bias.shape, jnp.float32), grad_qv_here, tp_rank * cols_here, 1
    )
    grad_qkv_w = jnp.einsum(
        "rd,rkc->kdc", normed_all, grad_proj, preferred_element_type=jnp.float32
    )
    grad_proj_rows = lax.all_to_all(grad_proj, "tp", 0, 2, tiled=True)
    grad_proj_rows, qkv_all = lax.optimization_barrier((grad_proj_rows, qkv_all))
    grad_normed = jnp.einsum(
        "rkc,kdc->rd", grad_proj_rows, qkv_all, preferred_element_type=jnp.float32
    )
    grad_in_norm, grad_ln1_gain, grad_ln1_bias = norm_backward(
        grad_normed, unit_one, inv_one, ln1_gain
    )
    grad_input = grad_middle + grad_in_norm
    grad_table = lax.dot_general(
        one_hot,
        grad_input,
        (((0,), (0,)), ((), ())),
        precision=HIGH,
        preferred_element_type=jnp.float32,
    )
    qkv_shard = lax.psum_scatter(grad_qkv_w, "fsdp", scatter_dimension=1, tiled=True)
    summed = lax.psum(
        (
            grad_ln1_gain,
            grad_ln1_bias,
            grad_qv_bias,
            grad_out_bias,
            grad_ln2_gain,
            grad_ln2_bias,
            grad_fc1_bias,
            grad_fc2_bias,
            grad_table,
        ),
        ("fsdp", "tp"),
    )
    return (
        result.astype(jnp.bfloat16),
        grad_input,
        qkv_shard,
        out_shard,
        fc1_shard,
        fc2_shard,
        summed[0],
        summed[1],
        summed[2],
        summed[3],
        summed[4],
        summed[5],
        summed[6],
        summed[7],
        summed[8],
    )


def solution(mesh):
    placed = (
        P(("fsdp", "tp"), None),
        P(("fsdp", "tp")),
        P("fsdp"),
        P(("fsdp", "tp"), None),
        P(None, "fsdp", "tp"),
        P("tp", "fsdp"),
        P("fsdp", "tp"),
        P("tp", "fsdp"),
        P(),
        P(),
        P(),
        P(),
        P(),
        P(),
        P(),
        P(),
        P(),
    )
    return jax.shard_map(
        on_device,
        mesh=mesh,
        in_specs=placed,
        out_specs=(
            P(("fsdp", "tp"), None),
            P(("fsdp", "tp"), None),
            P(None, "fsdp", "tp"),
            P("tp", "fsdp"),
            P("fsdp", "tp"),
            P("tp", "fsdp"),
            P(),
            P(),
            P(),
            P(),
            P(),
            P(),
            P(),
            P(),
            P(),
        ),
        check_vma=False,
    )
```

profile of v0, /device:TPU:0, one launch (start us, length us, event | category | flops | bytes accessed | tf_op | source)
XLA Modules:
  0.0 645.1 jit_solution(12459462399136723489)
XLA Ops:
  13.2 38.9 %all_gather.30 = bf16[3,768,192]{2,0,1:T(4,128)(2,1)S(1)} all-gather(bf16[3,96,192]{2,0,1:T(4,128)(2,1)S(1)} %copy.92), channel_id=1, replica_groups=mesh['fsdp'=8,'tp'=4] {'fsdp'}, dimensions={1}, use_global_device_ids=true | all-gather | bytes 995328 | tf_op jit(solution)/shard_map/all_gather | solution.py:145
  66.7 89.5 %while.27 = (s32[]{:T(128)}, bf16[4,512,3,64]{1,3,2,0:T(8,128)(2,1)S(1)}, f32[4,3,512]{2,1,0:T(4,128)S(1)}, s32[4]{0:T(128)S(1)}, s32[]{:T(128)}, /*index=5*/bf1...) while((s32[]{:T(128)}, ...), condition=%wide.region_5.6_spmd, body=%wide.region_2.5_spmd.sunk | while | flops 845251584 | bytes 43976836 | solution.py:71
  75.4 6.9 %fusion.130 = f32[3,512]{1,0:T(4,128)S(1)} fusion(f32[3,512,2048]{2,1,0:T(8,128)} %get-tuple-element.513, f32[3,512]{1,0:T(4,128)S(1)} %get-tuple-element.514, pred[512,2048]{1,0:T(8,128)(4,1)S(1)} %fusion.128), kind=kLoop, calls=%fused_computation.4.clone.1 | loop fusion | flops 12581376 | bytes 13643776 | tf_op jit(solution)/shard_map/while/body/eval_jaxpr/reduce_sum | solution.py:64
  82.3 6.8 %fusion.131 = bf16[4,512,3,64]{1,3,2,0:T(8,128)(2,1)S(1)} fusion(bf16[4,512,3,64]{1,3,2,0:T(8,128)(2,1)S(1)} %get-tuple-element.538, s32[]{:T(128)S(6)} %copy.135, bf16[2048,3,64]{0,2,1:T(8,128)(2,1)S(1)} %get-tuple-element.553, f32[3,512,2048]{2,1,0:T(8,128)} %get-tuple-element.513, f32[3,512]{1,0:T(4,128)S(1)} %fusion.130, ...), kind=kOutput, calls=%fused_computation.10.clone.1 | convolution fusion | flops 418480128 | bytes 14630916 | tf_op jit(solution)/shard_map/while/body/eval_jaxpr/hqk,khe->qhe/dot_general | solution.py:66
  97.9 6.8 %fusion.130 = f32[3,512]{1,0:T(4,128)S(1)} fusion(f32[3,512,2048]{2,1,0:T(8,128)} %get-tuple-element.513, f32[3,512]{1,0:T(4,128)S(1)} %get-tuple-element.514, pred[512,2048]{1,0:T(8,128)(4,1)S(1)} %fusion.128), kind=kLoop, calls=%fused_computation.4.clone.1 | loop fusion | flops 12581376 | bytes 13643776 | tf_op jit(solution)/shard_map/while/body/eval_jaxpr/reduce_sum | solution.py:64
  104.6 6.8 %fusion.131 = bf16[4,512,3,64]{1,3,2,0:T(8,128)(2,1)S(1)} fusion(bf16[4,512,3,64]{1,3,2,0:T(8,128)(2,1)S(1)} %get-tuple-element.538, s32[]{:T(128)S(6)} %copy.135, bf16[2048,3,64]{0,2,1:T(8,128)(2,1)S(1)} %get-tuple-element.553, f32[3,512,2048]{2,1,0:T(8,128)} %get-tuple-element.513, f32[3,512]{1,0:T(4,128)S(1)} %fusion.130, ...), kind=kOutput, calls=%fused_computation.10.clone.1 | convolution fusion | flops 418480128 | bytes 14630916 | tf_op jit(solution)/shard_map/while/body/eval_jaxpr/hqk,khe->qhe/dot_general | solution.py:66
  120.2 6.8 %fusion.130 = f32[3,512]{1,0:T(4,128)S(1)} fusion(f32[3,512,2048]{2,1,0:T(8,128)} %get-tuple-element.513, f32[3,512]{1,0:T(4,128)S(1)} %get-tuple-element.514, pred[512,2048]{1,0:T(8,128)(4,1)S(1)} %fusion.128), kind=kLoop, calls=%fused_computation.4.clone.1 | loop fusion | flops 12581376 | bytes 13643776 | tf_op jit(solution)/shard_map/while/body/eval_jaxpr/reduce_sum | solution.py:64
  127.0 6.8 %fusion.131 = bf16[4,512,3,64]{1,3,2,0:T(8,128)(2,1)S(1)} fusion(bf16[4,512,3,64]{1,3,2,0:T(8,128)(2,1)S(1)} %get-tuple-element.538, s32[]{:T(128)S(6)} %copy.135, bf16[2048,3,64]{0,2,1:T(8,128)(2,1)S(1)} %get-tuple-element.553, f32[3,512,2048]{2,1,0:T(8,128)} %get-tuple-element.513, f32[3,512]{1,0:T(4,128)S(1)} %fusion.130, ...), kind=kOutput, calls=%fused_computation.10.clone.1 | convolution fusion | flops 418480128 | bytes 14630916 | tf_op jit(solution)/shard_map/while/body/eval_jaxpr/hqk,khe->qhe/dot_general | solution.py:66
  142.6 6.8 %fusion.130 = f32[3,512]{1,0:T(4,128)S(1)} fusion(f32[3,512,2048]{2,1,0:T(8,128)} %get-tuple-element.513, f32[3,512]{1,0:T(4,128)S(1)} %get-tuple-element.514, pred[512,2048]{1,0:T(8,128)(4,1)S(1)} %fusion.128), kind=kLoop, calls=%fused_computation.4.clone.1 | loop fusion | flops 12581376 | bytes 13643776 | tf_op jit(solution)/shard_map/while/body/eval_jaxpr/reduce_sum | solution.py:64
  149.4 6.8 %fusion.131 = bf16[4,512,3,64]{1,3,2,0:T(8,128)(2,1)S(1)} fusion(bf16[4,512,3,64]{1,3,2,0:T(8,128)(2,1)S(1)} %get-tuple-element.538, s32[]{:T(128)S(6)} %copy.135, bf16[2048,3,64]{0,2,1:T(8,128)(2,1)S(1)} %get-tuple-element.553, f32[3,512,2048]{2,1,0:T(8,128)} %get-tuple-element.513, f32[3,512]{1,0:T(4,128)S(1)} %fusion.130, ...), kind=kOutput, calls=%fused_computation.10.clone.1 | convolution fusion | flops 418480128 | bytes 14630916 | tf_op jit(solution)/shard_map/while/body/eval_jaxpr/hqk,khe->qhe/dot_general | solution.py:66
  167.6 22.4 %all-gather.22.cloned.1.call-done = bf16[6144,96]{1,0:T(8,128)(2,1)} async-done(((bf16[192,96]{1,0:T(8,128)(2,1)}), bf16[6144,96]{1,0:T(8,128)(2,1)}) %all-gather.22.cloned.1.call-update) | async-done | bytes 1179664 | tf_op jit(solution)/shard_map/all_gather | solution.py:155
  214.3 12.4 %all-gather.14.cloned.1.call-done = bf16[2048,768]{1,0:T(8,128)(2,1)} async-done(((bf16[512,768]{1,0:T(8,128)(2,1)}), bf16[2048,768]{1,0:T(8,128)(2,1)}) %all-gather.14.cloned.1.call-update) | async-done | bytes 3145744 | tf_op jit(solution)/shard_map/all_gather | solution.py:190
  231.8 8.3 %convert_reduce_fusion = (f32[768]{0:T(1024)}, bf16[2048,768]{1,0:T(8,128)(2,1)S(1)}, bf16[2048,768]{1,0:T(8,128)(2,1)}) fusion(f32[2048,768]{1,0:T(8,128)S(1)} %fusion.71, f32[768]{0:T(1024)S(1)} %dynamic_slice.31, bf16[2048,768]{1,0:T(8,128)(2,1)S(1)} %copy-done.48, bf16[768,768]{0,1:T(8,128)(2,1)S(1)} %bitcast.200), kind=kOutput, calls=%fused_computation.64 | convolution fusion | flops 2455239936 | bytes 16914432 | tf_op jit(solution)/shard_map/dot_general | solution.py:31
  246.9 6.6 %convolution_convert_fusion = bf16[2048,768]{1,0:T(8,128)(2,1)} fusion(bf16[2048,768]{1,0:T(8,128)(2,1)} %get-tuple-element.391, bf16[768,768]{0,1:T(8,128)(2,1)} %bitcast.199), kind=kOutput, calls=%fused_computation.67 | convolution fusion | flops 2417491968 | bytes 7471104 | tf_op jit(solution)/shard_map/dot_general | solution.py:193
  253.6 8.6 %fusion.74 = f32[768,768]{1,0:T(8,128)} fusion(bf16[2048,768]{1,0:T(8,128)(2,1)} %get-tuple-element.391, bf16[2048,768]{1,0:T(8,128)(2,1)} %all-gather.12.cloned.1.call-done), kind=kOutput, calls=%fused_computation.134 | convolution fusion | flops 2415919104 | bytes 8650752 | tf_op jit(solution)/shard_map/dot_general | solution.py:37
  266.3 39.1 %reduce-scatter.7.cloned.1.call-done = f32[512,768]{1,0:T(8,128)} async-done(((f32[2048,768]{1,0:T(8,128)}), f32[512,768]{1,0:T(8,128)}) %reduce-scatter.7.cloned.1.call-update) | async-done | bytes 1572880 | tf_op jit(solution)/shard_map/reduce_scatter | solution.py:204
  327.2 13.3 %all-gather.16.cloned.1.call-done = bf16[2048,768]{1,0:T(8,128)(2,1)} async-done(((bf16[512,768]{1,0:T(8,128)(2,1)}), bf16[2048,768]{1,0:T(8,128)(2,1)}) %all-gather.16.cloned.1.call-update) | async-done | bytes 3145744 | tf_op jit(solution)/shard_map/all_gather | solution.py:216
  349.3 6.4 reshape.278
  360.2 137.4 %while.28 = (s32[]{:T(128)}, f32[2048,3,64]{0,2,1:T(8,128)}, f32[2048,3,64]{0,2,1:T(8,128)}, bf16[4,512,3,64]{1,3,2,0:T(8,128)(2,1)}, bf16[4,512,3,64]{1,3,2,0:T...) while((s32[]{:T(128)}, f32[2048,3,64]{0,2,1:T(8,128)}, ...), condition=%wide.region_13.14_spmd.clone, body=%wide.region_11.13_spmd.clone.sunk | while | flops 2064614400 | bytes 156684720 | solution.py:110
  433.8 6.4 fusion.144
  520.7 7.0 %copy.104 = bf16[2048,3,192]{2,1,0:T(4,128)(2,1)} copy(bf16[2048,3,192]{0,2,1:T(8,128)(2,1)} %pad_maximum_fusion.1) | data formatting | bytes 4718592 | tf_op jit(solution)/shard_map/optimization_barrier | solution.py:244
  537.8 43.1 %all-to-all-done.1 = bf16[2048,3,192]{2,1,0:T(4,128)(2,1)} async-done(((bf16[2048,3,192]{2,1,0:T(4,128)(2,1)}), bf16[2048,3,192]{2,1,0:T(4,128)(2,1)}, u32[]{:S(2)}, u32[]{:S(2)}) %all-to-all-start.1) | async-done | bytes 2359328 | tf_op jit(solution)/shard_map/all_to_all | solution.py:265
  581.0 7.2 %copy.106 = bf16[512,3,4,192]{0,3,2,1:T(8,128)(2,1)} copy(bf16[512,3,4,192]{3,1,0,2:T(4,128)(2,1)} %bitcast.23) | data formatting | bytes 4718592 | tf_op jit(solution)/shard_map/all_to_all | solution.py:265
  595.0 41.4 %all-reduce = (f32[768]{0:T(1024)}, f32[768]{0:T(1024)}, f32[2,768]{1,0:T(2,128)}, f32[768]{0:T(1024)}, f32[768]{0:T(1024)}, /*index=5*/f32[768]{0:T(1024)}, f32[3072]{0:T(1024)}, f32[768]{0:T(1024)}, f32[5,768]{1,0:T(8,128)}) all-reduce(f32[768]{0:T(1024)S(1)} %get-tuple-element.324, ...), channel_id=1, replica_groups=mesh['fsdp'=8,'tp'=4] {'fsdp','tp'}, use_global_device_ids=true, to_apply=%region_20.21 | all-reduce | flops 13056 | bytes 104448 | tf_op jit(solution)/shard_map/psum | solution.py:282
  (346 shorter events, 313.7 us)
Async XLA Ops:
  7.2 45.7 %all-gather.10.cloned.1.call-start = ((), (), s32[]{:S(2)}) async-start(), calls=%async_computation.6 | async-start | bytes 3932160 | tf_op jit(solution)/shard_map/all_gather | solution.py:154
  11.2 41.0 %copy-start.35 = (f32[512]{0:T(512)}, f32[512]{0:T(512)S(1)}, u32[]{:S(2)}) copy-start(f32[512]{0:T(512)S(1)} %add_rsqrt_fusion.1) | copy-start | bytes 6148
  12.4 144.6 %all-gather.20.cloned.1.call-start = ((), (), s32[]{:S(2)}) async-start(), calls=%async_computation.14 | async-start | bytes 2654208 | tf_op jit(solution)/shard_map/all_gather | solution.py:167
  52.9 108.5 %all-gather.12.cloned.1.call-start = ((), (), s32[]{:S(2)}) async-start(), calls=%async_computation.7 | async-start | bytes 3932160 | tf_op jit(solution)/shard_map/all_gather | solution.py:169
  53.7 136.3 %all-gather.22.cloned.1.call-start = ((), (), s32[]{:S(2)}) async-start(), calls=%async_computation.15 | async-start | bytes 1622016 | tf_op jit(solution)/shard_map/all_gather | solution.py:155
  162.4 32.2 %all-to-all-start = ((bf16[4,512,192]{1,2,0:T(8,128)(2,1)}), bf16[4,512,192]{1,2,0:T(8,128)(2,1)}, u32[]{:S(2)}, u32[]{:S(2)}) async-start(bf16[4,512,192]{1,2,0:T(8,128)(2,1)} %bitcast.141), calls=%async_computation | async-start | bytes 1572864 | tf_op jit(solution)/shard_map/all_to_all | solution.py:184
  166.6 60.2 %all-gather.14.cloned.1.call-start = ((), (), s32[]{:S(2)}) async-start(), calls=%async_computation.8 | async-start | bytes 3932160 | tf_op jit(solution)/shard_map/all_gather | solution.py:190
  197.5 110.9 %copy-start.8 = (f32[512,768]{1,0:T(8,128)}, f32[512,768]{1,0:T(8,128)S(1)}, u32[]{:S(2)}) copy-start(f32[512,768]{1,0:T(8,128)S(1)} %get-tuple-element.400) | copy-start | bytes 4718596
  199.1 106.4 %reduce-scatter.7.cloned.1.call-start = ((), (), s32[]{:S(2)}) async-start(), calls=%async_computation.9 | async-start | bytes 7864320 | tf_op jit(solution)/shard_map/reduce_scatter | solution.py:204
  231.8 10.1 %copy-start.27 = (bf16[768,768]{1,0:T(8,128)(2,1)S(1)}, bf16[768,768]{1,0:T(8,128)(2,1)}, u32[]{:S(2)}) copy-start(bf16[768,768]{1,0:T(8,128)(2,1)} %reshape_reshape.11) | copy-start | bytes 3538948
  246.5 94.0 %all-gather.16.cloned.1.call-start = ((), (), s32[]{:S(2)}) async-start(), calls=%async_computation.10 | async-start | bytes 3932160 | tf_op jit(solution)/shard_map/all_gather | solution.py:216
  253.6 8.7 %copy-start.49 = (bf16[2048,768]{1,0:T(8,128)(2,1)S(1)}, bf16[2048,768]{1,0:T(8,128)(2,1)}, u32[]{:S(2)}) copy-start(bf16[2048,768]{1,0:T(8,128)(2,1)} %all-gather.14.cloned.1.call-done) | copy-start | bytes 9437188
  253.6 8.7 %copy-start.52 = (bf16[2048,768]{1,0:T(8,128)(2,1)S(1)}, bf16[2048,768]{1,0:T(8,128)(2,1)}, u32[]{:S(2)}) copy-start(bf16[2048,768]{1,0:T(8,128)(2,1)} %copy-done.51) | copy-start | bytes 9437188
  311.8 192.1 %reduce-scatter.9.cloned.1.call-start = ((), (), s32[]{:S(2)}) async-start(), calls=%async_computation.11 | async-start | bytes 3932160 | tf_op jit(solution)/shard_map/reduce_scatter | solution.py:220
  322.0 18.5 %copy-start.16 = (bf16[24,8,4,512]{3,1,2,0:T(8,128)(2,1)S(1)}, bf16[24,8,4,512]{3,1,2,0:T(8,128)(2,1)}, u32[]{:S(2)}) copy-start(bf16[24,8,4,512]{3,1,2,0:T(8,128)(2,1)} %copy-done.15) | copy-start | bytes 2359300
  343.2 163.1 %reduce-scatter.11.cloned.1.call-start = ((), (), s32[]{:S(2)}) async-start(), calls=%async_computation.12 | async-start | bytes 5971968 | tf_op jit(solution)/shard_map/reduce_scatter | solution.py:231
  355.7 232.4 %all-gather.18.cloned.1.call-start = ((), (), s32[]{:S(2)}) async-start(), calls=%async_computation.13 | async-start | bytes 4423680 | tf_op jit(solution)/shard_map/all_gather | solution.py:168
  356.3 280.1 %reduce-scatter.13.cloned.1.call-start = ((), (), s32[]{:S(2)}) async-start(), calls=%async_computation.16 | async-start | bytes 2211840
  527.7 53.2 %all-to-all-start.1 = ((bf16[2048,3,192]{2,1,0:T(4,128)(2,1)}), bf16[2048,3,192]{2,1,0:T(4,128)(2,1)}, u32[]{:S(2)}, u32[]{:S(2)}) async-start(bf16[2048,3,192]{2,1,0:T(4,128)(2,1)} %copy.104), calls=%async_computation.4 | async-start | bytes 8388608 | tf_op jit(solution)/shard_map/all_to_all | solution.py:265
  580.9 7.2 %copy-start.34 = (f32[512]{0:T(512)S(1)}, f32[512]{0:T(512)}, u32[]{:S(2)}) copy-start(f32[512]{0:T(512)} %copy-done.33) | copy-start | bytes 6148
  580.9 7.2 %copy-start.36 = (f32[512]{0:T(512)S(1)}, f32[512]{0:T(512)}, u32[]{:S(2)}) copy-start(f32[512]{0:T(512)} %copy-done.35) | copy-start | bytes 6148
  581.0 7.2 %copy-start.42 = (f32[768]{0:T(1024)S(1)}, f32[768]{0:T(1024)}, u32[]{:S(2)}) copy-start(f32[768]{0:T(1024)} %param.29) | copy-start | bytes 9220
  593.7 44.7 %copy-start.1 = (f32[5,768]{1,0:T(8,128)S(1)}, f32[5,768]{1,0:T(8,128)}, u32[]{:S(2)}) copy-start(f32[5,768]{1,0:T(8,128)} %param.37) | copy-start | bytes 46084
  594.3 44.1 %copy-start.17 = (f32[512,768]{1,0:T(8,128)}, f32[512,768]{1,0:T(8,128)S(1)}, u32[]{:S(2)}) copy-start(f32[512,768]{1,0:T(8,128)S(1)} %multiply_add_fusion) | copy-start | bytes 4718596
  (66 other events, 260.7 us)
Sparse Core Ops, SparseCore 0:
  12.5 31.2 all-gather.9
  53.0 50.5 all-gather.19
  105.2 27.0 all-gather.11
  135.0 54.9 all-gather.21
  199.2 27.4 all-gather.13
  246.6 58.8 reduce-scatter.6
  312.0 28.4 all-gather.15
  343.4 37.8 reduce-scatter.8
  384.9 104.4 reduce-scatter.10
  490.8 30.3 all-gather.17
  524.7 67.3 reduce-scatter.12
where the time goes:
time: 650 us; the launch traced here: 645 us
  matrix products  216 us (33%)
  waiting for transfers between devices  132 us (20%)
  local copies, waits for them, and re-layouts  97.2 us (15%)
  other arithmetic  93.3 us (14%)
  blocking collectives  80.3 us (12%)
  between operations  14.8 us (2%)
  starting transfers between devices  10.7 us (2%)
    all_to_all x1, waiting for transfers between devices, on_device(): grad_proj_rows = lax.all_to_all(grad_proj, 'tp', 0, 2, tiled=True)  43.1 us
    psum x1, blocking collectives, on_device(): lax.psum((grad_ln1_gain, grad_ln1_bias, grad_qv_bias, grad_out_bias, grad...  41.4 us
    reduce_scatter x1, waiting for transfers between devices, on_device(): lax.psum_scatter(matmul_nt(grad_before, fc1_part), 'tp', scatter_dimensio...  39.1 us
    all_gather x1, blocking collectives, on_device(): qkv_cols = lax.all_gather(qkv_weight, 'fsdp', axis=1, tiled=True)  38.9 us
    dot_general x8, matrix products, block_scores(): jnp.einsum('qhe,khe->hqk', query_block, keys_all, preferred_element_type=...  36.4 us
    reduce_sum x4, other arithmetic, one_block(): total_mass = jnp.sum(expo, axis=-1, keepdims=True)  27.2 us
    dot_general x4, matrix products, one_block(): jnp.einsum('hqk,khe->qhe', probs_low, values_all, preferred_element_type=...  27.1 us
    convert_element_type x4, other arithmetic, one_block(): grad_scores = (probs * (grad_probs - inner_sum)).astype(jnp.bfloat16)  25.2 us
  transfers between devices with their start and end apart: 13, of which 5 were waited for; matrix products, arithmetic and copies ran while one was open for 57% of the time, Pallas kernels for 0%

commit v1 on v0

--- a/solution.py
+++ b/solution.py
@@ -262,7 +262,10 @@
     grad_qkv_w = jnp.einsum(
         "rd,rkc->kdc", normed_all, grad_proj, preferred_element_type=jnp.float32
     )
-    grad_proj_rows = lax.all_to_all(grad_proj, "tp", 0, 2, tiled=True)
+    grad_proj_rows = jnp.concatenate(
+        lax.all_to_all(jnp.stack(jnp.split(grad_proj, lax.axis_size("tp"), axis=0)), "tp", 0, 0),
+        axis=2,
+    )
     grad_proj_rows, qkv_all = lax.optimization_barrier((grad_proj_rows, qkv_all))
     grad_normed = jnp.einsum(
         "rkc,kdc->rd", grad_proj_rows, qkv_all, preferred_element_type=jnp.float32

time: 650 us -> 624 us (0.960)
  waiting for transfers between devices: 132 us -> 110 us
    all_to_all x1, waiting for transfers between devices: 43.1 us -> 21.2 us  [on_device(): lax.all_to_all(jnp.stack(jnp.split(grad_proj, lax.axis_size('tp'), axis=0...]
    all_to_all x1 -> x0, local copies, waits for them, and re-layouts: 7.15 us -> none  [on_device(): grad_proj_rows = lax.all_to_all(grad_proj, 'tp', 0, 2, tiled=True)]
    optimization_barrier x1 -> x0, local copies, waits for them, and re-layouts: 6.96 us -> none  [on_device(): lax.optimization_barrier((grad_proj, result, dense_summed))]
  transfers between devices with their start and end apart: 13 -> 13, of which waited for: 5 -> 5; matrix products, arithmetic and copies ran while one was open for 57% -> 58% of each run, Pallas kernels for 0% -> 0%
where the time goes in v1:
time: 624 us; the launch traced here: 619 us
  matrix products  216 us (35%)
  waiting for transfers between devices  110 us (18%)
  other arithmetic  95.2 us (15%)
  local copies, waits for them, and re-layouts  91.9 us (15%)
  blocking collectives  80.6 us (13%)
  between operations  14.8 us (2%)
  starting transfers between devices  9.46 us (2%)
    psum x1, blocking collectives, on_device(): lax.psum((grad_ln1_gain, grad_ln1_bias, grad_qv_bias, grad_out_bias, grad...  41.7 us
    reduce_scatter x1, waiting for transfers between devices, on_device(): lax.psum_scatter(matmul_nt(grad_before, fc1_part), 'tp', scatter_dimensio...  39.1 us
    all_gather x1, blocking collectives, on_device(): qkv_cols = lax.all_gather(qkv_weight, 'fsdp', axis=1, tiled=True)  38.9 us
    dot_general x8, matrix products, block_scores(): jnp.einsum('qhe,khe->hqk', query_block, keys_all, preferred_element_type=...  36.4 us
    reduce_sum x4, other arithmetic, one_block(): total_mass = jnp.sum(expo, axis=-1, keepdims=True)  27.3 us
    dot_general x4, matrix products, one_block(): jnp.einsum('hqk,khe->qhe', probs_low, values_all, preferred_element_type=...  27.1 us
    convert_element_type x4, other arithmetic, one_block(): grad_scores = (probs * (grad_probs - inner_sum)).astype(jnp.bfloat16)  25.3 us
    dot_general x4, matrix products, one_block(): jnp.einsum('qhe,khe->hqk', grad_block, values_all, preferred_element_type...  24.6 us
  transfers between devices with their start and end apart: 13, of which 5 were waited for; matrix products, arithmetic and copies ran while one was open for 58% of the time, Pallas kernels for 0%

profile of v1, /device:TPU:0, one launch (start us, length us, event | category | flops | bytes accessed | tf_op | source)
XLA Modules:
  0.0 618.9 jit_solution(5381323511607898488)
XLA Ops:
  13.2 38.9 %all_gather.30 = bf16[3,768,192]{2,0,1:T(4,128)(2,1)S(1)} all-gather(bf16[3,96,192]{2,0,1:T(4,128)(2,1)S(1)} %copy.72), channel_id=1, replica_groups=mesh['fsdp'=8,'tp'=4] {'fsdp'}, dimensions={1}, use_global_device_ids=true | all-gather | bytes 995328 | tf_op jit(solution)/shard_map/all_gather | solution.py:145
  66.7 89.6 %while.27 = (s32[]{:T(128)}, bf16[4,512,3,64]{1,3,2,0:T(8,128)(2,1)S(1)}, f32[4,3,512]{2,1,0:T(4,128)S(1)}, s32[4]{0:T(128)S(1)}, s32[]{:T(128)}, /*index=5*/bf1...) while((s32[]{:T(128)}, ...), condition=%wide.region_5.6_spmd, body=%wide.region_2.5_spmd.sunk | while | flops 845251584 | bytes 43976836 | solution.py:71
  75.4 7.0 %fusion.130 = f32[3,512]{1,0:T(4,128)S(1)} fusion(f32[3,512,2048]{2,1,0:T(8,128)} %get-tuple-element.491, f32[3,512]{1,0:T(4,128)S(1)} %get-tuple-element.492, pred[512,2048]{1,0:T(8,128)(4,1)S(1)} %fusion.128), kind=kLoop, calls=%fused_computation.4.clone.1 | loop fusion | flops 12581376 | bytes 13643776 | tf_op jit(solution)/shard_map/while/body/eval_jaxpr/reduce_sum | solution.py:64
  82.4 6.8 %fusion.131 = bf16[4,512,3,64]{1,3,2,0:T(8,128)(2,1)S(1)} fusion(bf16[4,512,3,64]{1,3,2,0:T(8,128)(2,1)S(1)} %get-tuple-element.516, s32[]{:T(128)S(6)} %copy.111, bf16[2048,3,64]{0,2,1:T(8,128)(2,1)S(1)} %get-tuple-element.531, f32[3,512,2048]{2,1,0:T(8,128)} %get-tuple-element.491, f32[3,512]{1,0:T(4,128)S(1)} %fusion.130, ...), kind=kOutput, calls=%fused_computation.10.clone.1 | convolution fusion | flops 418480128 | bytes 14630916 | tf_op jit(solution)/shard_map/while/body/eval_jaxpr/hqk,khe->qhe/dot_general | solution.py:66
  98.0 6.8 %fusion.130 = f32[3,512]{1,0:T(4,128)S(1)} fusion(f32[3,512,2048]{2,1,0:T(8,128)} %get-tuple-element.491, f32[3,512]{1,0:T(4,128)S(1)} %get-tuple-element.492, pred[512,2048]{1,0:T(8,128)(4,1)S(1)} %fusion.128), kind=kLoop, calls=%fused_computation.4.clone.1 | loop fusion | flops 12581376 | bytes 13643776 | tf_op jit(solution)/shard_map/while/body/eval_jaxpr/reduce_sum | solution.py:64
  104.7 6.8 %fusion.131 = bf16[4,512,3,64]{1,3,2,0:T(8,128)(2,1)S(1)} fusion(bf16[4,512,3,64]{1,3,2,0:T(8,128)(2,1)S(1)} %get-tuple-element.516, s32[]{:T(128)S(6)} %copy.111, bf16[2048,3,64]{0,2,1:T(8,128)(2,1)S(1)} %get-tuple-element.531, f32[3,512,2048]{2,1,0:T(8,128)} %get-tuple-element.491, f32[3,512]{1,0:T(4,128)S(1)} %fusion.130, ...), kind=kOutput, calls=%fused_computation.10.clone.1 | convolution fusion | flops 418480128 | bytes 14630916 | tf_op jit(solution)/shard_map/while/body/eval_jaxpr/hqk,khe->qhe/dot_general | solution.py:66
  120.3 6.8 %fusion.130 = f32[3,512]{1,0:T(4,128)S(1)} fusion(f32[3,512,2048]{2,1,0:T(8,128)} %get-tuple-element.491, f32[3,512]{1,0:T(4,128)S(1)} %get-tuple-element.492, pred[512,2048]{1,0:T(8,128)(4,1)S(1)} %fusion.128), kind=kLoop, calls=%fused_computation.4.clone.1 | loop fusion | flops 12581376 | bytes 13643776 | tf_op jit(solution)/shard_map/while/body/eval_jaxpr/reduce_sum | solution.py:64
  127.1 6.8 %fusion.131 = bf16[4,512,3,64]{1,3,2,0:T(8,128)(2,1)S(1)} fusion(bf16[4,512,3,64]{1,3,2,0:T(8,128)(2,1)S(1)} %get-tuple-element.516, s32[]{:T(128)S(6)} %copy.111, bf16[2048,3,64]{0,2,1:T(8,128)(2,1)S(1)} %get-tuple-element.531, f32[3,512,2048]{2,1,0:T(8,128)} %get-tuple-element.491, f32[3,512]{1,0:T(4,128)S(1)} %fusion.130, ...), kind=kOutput, calls=%fused_computation.10.clone.1 | convolution fusion | flops 418480128 | bytes 14630916 | tf_op jit(solution)/shard_map/while/body/eval_jaxpr/hqk,khe->qhe/dot_general | solution.py:66
  142.7 6.8 %fusion.130 = f32[3,512]{1,0:T(4,128)S(1)} fusion(f32[3,512,2048]{2,1,0:T(8,128)} %get-tuple-element.491, f32[3,512]{1,0:T(4,128)S(1)} %get-tuple-element.492, pred[512,2048]{1,0:T(8,128)(4,1)S(1)} %fusion.128), kind=kLoop, calls=%fused_computation.4.clone.1 | loop fusion | flops 12581376 | bytes 13643776 | tf_op jit(solution)/shard_map/while/body/eval_jaxpr/reduce_sum | solution.py:64
  149.5 6.8 %fusion.131 = bf16[4,512,3,64]{1,3,2,0:T(8,128)(2,1)S(1)} fusion(bf16[4,512,3,64]{1,3,2,0:T(8,128)(2,1)S(1)} %get-tuple-element.516, s32[]{:T(128)S(6)} %copy.111, bf16[2048,3,64]{0,2,1:T(8,128)(2,1)S(1)} %get-tuple-element.531, f32[3,512,2048]{2,1,0:T(8,128)} %get-tuple-element.491, f32[3,512]{1,0:T(4,128)S(1)} %fusion.130, ...), kind=kOutput, calls=%fused_computation.10.clone.1 | convolution fusion | flops 418480128 | bytes 14630916 | tf_op jit(solution)/shard_map/while/body/eval_jaxpr/hqk,khe->qhe/dot_general | solution.py:66
  167.7 22.4 %all-gather.22.cloned.1.call-done = bf16[6144,96]{1,0:T(8,128)(2,1)} async-done(((bf16[192,96]{1,0:T(8,128)(2,1)}), bf16[6144,96]{1,0:T(8,128)(2,1)}) %all-gather.22.cloned.1.call-update) | async-done | bytes 1179664 | tf_op jit(solution)/shard_map/all_gather | solution.py:155
  214.4 12.4 %all-gather.14.cloned.1.call-done = bf16[2048,768]{1,0:T(8,128)(2,1)} async-done(((bf16[512,768]{1,0:T(8,128)(2,1)}), bf16[2048,768]{1,0:T(8,128)(2,1)}) %all-gather.14.cloned.1.call-update) | async-done | bytes 3145744 | tf_op jit(solution)/shard_map/all_gather | solution.py:190
  231.9 8.3 %convert_reduce_fusion = (f32[768]{0:T(1024)}, bf16[2048,768]{1,0:T(8,128)(2,1)S(1)}, bf16[2048,768]{1,0:T(8,128)(2,1)}) fusion(f32[2048,768]{1,0:T(8,128)S(1)} %fusion.71, f32[768]{0:T(1024)S(1)} %dynamic_slice.31, bf16[2048,768]{1,0:T(8,128)(2,1)S(1)} %copy-done.48, bf16[768,768]{0,1:T(8,128)(2,1)S(1)} %bitcast.206), kind=kOutput, calls=%fused_computation.64 | convolution fusion | flops 2455239936 | bytes 16914432 | tf_op jit(solution)/shard_map/dot_general | solution.py:31
  247.1 6.6 %convolution_convert_fusion = bf16[2048,768]{1,0:T(8,128)(2,1)} fusion(bf16[2048,768]{1,0:T(8,128)(2,1)} %get-tuple-element.365, bf16[768,768]{0,1:T(8,128)(2,1)} %bitcast.205), kind=kOutput, calls=%fused_computation.67 | convolution fusion | flops 2417491968 | bytes 7471104 | tf_op jit(solution)/shard_map/dot_general | solution.py:193
  253.7 8.7 %fusion.74 = f32[768,768]{1,0:T(8,128)} fusion(bf16[2048,768]{1,0:T(8,128)(2,1)} %get-tuple-element.365, bf16[2048,768]{1,0:T(8,128)(2,1)} %all-gather.12.cloned.1.call-done), kind=kOutput, calls=%fused_computation.139 | convolution fusion | flops 2415919104 | bytes 8650752 | tf_op jit(solution)/shard_map/dot_general | solution.py:37
  266.5 39.1 %reduce-scatter.7.cloned.1.call-done = f32[512,768]{1,0:T(8,128)} async-done(((f32[2048,768]{1,0:T(8,128)}), f32[512,768]{1,0:T(8,128)}) %reduce-scatter.7.cloned.1.call-update) | async-done | bytes 1572880 | tf_op jit(solution)/shard_map/reduce_scatter | solution.py:204
  327.3 13.3 %all-gather.16.cloned.1.call-done = bf16[2048,768]{1,0:T(8,128)(2,1)} async-done(((bf16[512,768]{1,0:T(8,128)(2,1)}), bf16[2048,768]{1,0:T(8,128)(2,1)}) %all-gather.16.cloned.1.call-update) | async-done | bytes 3145744 | tf_op jit(solution)/shard_map/all_gather | solution.py:216
  349.5 6.4 %reshape.284 = f32[1728,768]{1,0:T(8,128)} reshape(f32[8,165888]{1,0:T(8,128)} %pad_maximum_fusion) | data formatting | bytes 10616832 | tf_op jit(solution)/shard_map/reshape | solution.py:232
  360.4 137.5 %while.28 = (s32[]{:T(128)}, f32[2048,3,64]{0,2,1:T(8,128)}, f32[2048,3,64]{0,2,1:T(8,128)}, bf16[4,512,3,64]{1,3,2,0:T(8,128)(2,1)}, bf16[4,512,3,64]{1,3,2,0:T...) while((s32[]{:T(128)}, f32[2048,3,64]{0,2,1:T(8,128)}, ...), condition=%wide.region_13.14_spmd.clone, body=%wide.region_11.13_spmd.clone.sunk | while | flops 2064614400 | bytes 156684720 | solution.py:110
  399.2 6.3 %fusion.144 = f32[2048,3,64]{0,2,1:T(8,128)} fusion(f32[3,512,2048]{2,1,0:T(8,128)S(1)} %fusion.141, f32[3,512]{1,0:T(4,128)S(1)} %dynamic-slice_bitcast_fusion.2, pred[512,2048]{1,0:T(8,128)(4,1)S(1)} %fusion.142, f32[2048,3,64]{0,2,1:T(8,128)} %get-tuple-element.548, pred[]{:T(512)S(6)} %compare.3, ...), kind=kOutput, calls=%fused_computation.32.clone.1 | convolution fusion | flops 416022528 | bytes 16982020 | tf_op jit(solution)/shard_map/while/body/eval_jaxpr/hqk,qhe->khe/dot_general | solution.py:88
  434.0 6.4 %fusion.144 = f32[2048,3,64]{0,2,1:T(8,128)} fusion(f32[3,512,2048]{2,1,0:T(8,128)S(1)} %fusion.141, f32[3,512]{1,0:T(4,128)S(1)} %dynamic-slice_bitcast_fusion.2, pred[512,2048]{1,0:T(8,128)(4,1)S(1)} %fusion.142, f32[2048,3,64]{0,2,1:T(8,128)} %get-tuple-element.548, pred[]{:T(512)S(6)} %compare.3, ...), kind=kOutput, calls=%fused_computation.32.clone.1 | convolution fusion | flops 416022528 | bytes 16982020 | tf_op jit(solution)/shard_map/while/body/eval_jaxpr/hqk,qhe->khe/dot_general | solution.py:88
  468.8 6.3 %fusion.144 = f32[2048,3,64]{0,2,1:T(8,128)} fusion(f32[3,512,2048]{2,1,0:T(8,128)S(1)} %fusion.141, f32[3,512]{1,0:T(4,128)S(1)} %dynamic-slice_bitcast_fusion.2, pred[512,2048]{1,0:T(8,128)(4,1)S(1)} %fusion.142, f32[2048,3,64]{0,2,1:T(8,128)} %get-tuple-element.548, pred[]{:T(512)S(6)} %compare.3, ...), kind=kOutput, calls=%fused_computation.32.clone.1 | convolution fusion | flops 416022528 | bytes 16982020 | tf_op jit(solution)/shard_map/while/body/eval_jaxpr/hqk,qhe->khe/dot_general | solution.py:88
  535.7 21.2 %all-to-all-done.1 = bf16[4,512,3,192]{1,3,2,0:T(8,128)(2,1)S(1)} async-done(((bf16[4,512,3,192]{1,3,2,0:T(8,128)(2,1)}), bf16[4,512,3,192]{1,3,2,0:T(8,128)(2,1)S(1)}, u32[]{:S(2)}, u32[]{:S(2)}) %all-to-all-start.1) | async-done | bytes 2359328 | tf_op jit(solution)/shard_map/all_to_all | solution.py:266
  568.6 41.7 %all-reduce = (f32[768]{0:T(1024)}, f32[768]{0:T(1024)}, f32[2,768]{1,0:T(2,128)}, f32[768]{0:T(1024)}, f32[768]{0:T(1024)}, /*index=5*/f32[768]{0:T(1024)}, f32[3072]{0:T(1024)}, f32[768]{0:T(1024)}, f32[5,768]{1,0:T(8,128)}) all-reduce(f32[768]{0:T(1024)S(1)} %get-tuple-element.298, ...), channel_id=1, replica_groups=mesh['fsdp'=8,'tp'=4] {'fsdp','tp'}, use_global_device_ids=true, to_apply=%region_20.21 | all-reduce | flops 13056 | bytes 104448 | tf_op jit(solution)/shard_map/psum | solution.py:285
  (347 shorter events, 310.5 us)
Async XLA Ops:
  7.2 45.7 %all-gather.10.cloned.1.call-start = ((), (), s32[]{:S(2)}) async-start(), calls=%async_computation.6 | async-start | bytes 3932160 | tf_op jit(solution)/shard_map/all_gather | solution.py:154
  11.2 41.0 %copy-start.35 = (f32[512]{0:T(512)}, f32[512]{0:T(512)S(1)}, u32[]{:S(2)}) copy-start(f32[512]{0:T(512)S(1)} %add_rsqrt_fusion.1) | copy-start | bytes 6148
  12.4 144.7 %all-gather.20.cloned.1.call-start = ((), (), s32[]{:S(2)}) async-start(), calls=%async_computation.14 | async-start | bytes 2654208 | tf_op jit(solution)/shard_map/all_gather | solution.py:167
  52.9 108.6 %all-gather.12.cloned.1.call-start = ((), (), s32[]{:S(2)}) async-start(), calls=%async_computation.7 | async-start | bytes 3932160 | tf_op jit(solution)/shard_map/all_gather | solution.py:169
  53.7 136.4 %all-gather.22.cloned.1.call-start = ((), (), s32[]{:S(2)}) async-start(), calls=%async_computation.15 | async-start | bytes 1622016 | tf_op jit(solution)/shard_map/all_gather | solution.py:155
  162.5 32.2 %all-to-all-start = ((bf16[4,512,192]{1,2,0:T(8,128)(2,1)}), bf16[4,512,192]{1,2,0:T(8,128)(2,1)}, u32[]{:S(2)}, u32[]{:S(2)}) async-start(bf16[4,512,192]{1,2,0:T(8,128)(2,1)} %bitcast.146), calls=%async_computation | async-start | bytes 1572864 | tf_op jit(solution)/shard_map/all_to_all | solution.py:184
  166.7 60.1 %all-gather.14.cloned.1.call-start = ((), (), s32[]{:S(2)}) async-start(), calls=%async_computation.8 | async-start | bytes 3932160 | tf_op jit(solution)/shard_map/all_gather | solution.py:190
  197.6 110.9 %copy-start.8 = (f32[512,768]{1,0:T(8,128)}, f32[512,768]{1,0:T(8,128)S(1)}, u32[]{:S(2)}) copy-start(f32[512,768]{1,0:T(8,128)S(1)} %get-tuple-element.378) | copy-start | bytes 4718596
  199.2 106.4 %reduce-scatter.7.cloned.1.call-start = ((), (), s32[]{:S(2)}) async-start(), calls=%async_computation.9 | async-start | bytes 7864320 | tf_op jit(solution)/shard_map/reduce_scatter | solution.py:204
  231.9 10.1 %copy-start.27 = (bf16[768,768]{1,0:T(8,128)(2,1)S(1)}, bf16[768,768]{1,0:T(8,128)(2,1)}, u32[]{:S(2)}) copy-start(bf16[768,768]{1,0:T(8,128)(2,1)} %reshape_reshape.11) | copy-start | bytes 3538948
  246.6 94.0 %all-gather.16.cloned.1.call-start = ((), (), s32[]{:S(2)}) async-start(), calls=%async_computation.10 | async-start | bytes 3932160 | tf_op jit(solution)/shard_map/all_gather | solution.py:216
  253.7 8.7 %copy-start.49 = (bf16[2048,768]{1,0:T(8,128)(2,1)S(1)}, bf16[2048,768]{1,0:T(8,128)(2,1)}, u32[]{:S(2)}) copy-start(bf16[2048,768]{1,0:T(8,128)(2,1)} %all-gather.14.cloned.1.call-done) | copy-start | bytes 9437188
  253.7 8.7 %copy-start.52 = (bf16[2048,768]{1,0:T(8,128)(2,1)S(1)}, bf16[2048,768]{1,0:T(8,128)(2,1)}, u32[]{:S(2)}) copy-start(bf16[2048,768]{1,0:T(8,128)(2,1)} %copy-done.51) | copy-start | bytes 9437188
  312.0 192.3 %reduce-scatter.9.cloned.1.call-start = ((), (), s32[]{:S(2)}) async-start(), calls=%async_computation.11 | async-start | bytes 3932160 | tf_op jit(solution)/shard_map/reduce_scatter | solution.py:220
  322.2 18.5 %copy-start.17 = (bf16[24,8,4,512]{3,1,2,0:T(8,128)(2,1)S(1)}, bf16[24,8,4,512]{3,1,2,0:T(8,128)(2,1)}, u32[]{:S(2)}) copy-start(bf16[24,8,4,512]{3,1,2,0:T(8,128)(2,1)} %copy-done.16) | copy-start | bytes 2359300
  343.4 163.3 %reduce-scatter.11.cloned.1.call-start = ((), (), s32[]{:S(2)}) async-start(), calls=%async_computation.12 | async-start | bytes 5971968 | tf_op jit(solution)/shard_map/reduce_scatter | solution.py:231
  355.9 205.8 %all-gather.18.cloned.1.call-start = ((), (), s32[]{:S(2)}) async-start(), calls=%async_computation.13 | async-start | bytes 4423680 | tf_op jit(solution)/shard_map/all_gather | solution.py:168
  356.5 253.8 %reduce-scatter.13.cloned.1.call-start = ((), (), s32[]{:S(2)}) async-start(), calls=%async_computation.16 | async-start | bytes 2211840
  418.0 5.9 copy-start.2
  428.1 5.9 copy-start.4
  487.6 5.9 copy-start.2
  524.7 32.2 %all-to-all-start.1 = ((bf16[4,512,3,192]{1,3,2,0:T(8,128)(2,1)}), bf16[4,512,3,192]{1,3,2,0:T(8,128)(2,1)S(1)}, u32[]{:S(2)}, u32[]{:S(2)}) async-start(bf16[4,512,3,192]{1,3,2,0:T(8,128)(2,1)} %pad_maximum_fusion.2), calls=%async_computation.4 | async-start | bytes 4718592 | tf_op jit(solution)/shard_map/all_to_all | solution.py:266
  567.2 44.9 %copy-start.1 = (f32[5,768]{1,0:T(8,128)S(1)}, f32[5,768]{1,0:T(8,128)}, u32[]{:S(2)}) copy-start(f32[5,768]{1,0:T(8,128)} %param.37) | copy-start | bytes 46084
  567.9 44.3 %copy-start.18 = (f32[512,768]{1,0:T(8,128)}, f32[512,768]{1,0:T(8,128)S(1)}, u32[]{:S(2)}) copy-start(f32[512,768]{1,0:T(8,128)S(1)} %multiply_add_fusion) | copy-start | bytes 4718596
  (66 other events, 242.4 us)
Sparse Core Ops, SparseCore 0:
  12.5 31.2 all-gather.9
  53.0 50.7 all-gather.19
  105.4 27.0 all-gather.11
  135.1 54.8 all-gather.21
  199.3 27.4 all-gather.13
  246.7 58.8 reduce-scatter.6
  312.1 28.4 all-gather.15
  343.5 37.8 reduce-scatter.8
  385.0 104.4 reduce-scatter.10
  490.9 30.3 all-gather.17
  524.8 67.6 reduce-scatter.12
